TPU v7x, 128 devices: a whole 4x4x4 slice. The times are simulated.
128 devices in a mesh: section: 4 (over z), dp: 8 (over y, core), mp: 4 (over x).
Axes of the slice: x: 4, y: 4, z: 4, core: 2. Of those that a mesh axis runs over, the one named last changes fastest.
Arguments:
- text: bfloat16 [4, 4096, 4096], P('section', ('dp', 'mp')), may hold values from -6 to 6
- patches: bfloat16 [16384, 1024], P(('section', 'dp')), may hold values from -6 to 6
- segments: int32 [4, 8, 512], P('section', 'dp'), may hold values from 0 to 3, never falling along the last dimension, each value on 1 to 256 neighbouring positions
- loss_mask: int32 [4, 4096], P('section', ('dp', 'mp')), may hold values from 0 to 1, as said below
- tile_batch: int32 [8, 8], P('dp'), may hold values from 0 to 3, as said below
- tile_offset: int32 [8, 8], P('dp'), may hold values from 0 to 448, as said below
- attn_gain: float32 [4, 4096], P('section'), may hold values from 0.5 to 2
- w_query: bfloat16 [4, 4096, 2048], P('section', None, 'mp'), may hold values from -0.09375 to 0.09375
- w_kv: bfloat16 [4, 2, 4096, 512], P('section', None, None, 'mp'), may hold values from -0.09375 to 0.09375
- w_out: bfloat16 [4, 2048, 4096], P('section', 'mp'), may hold values from -0.125 to 0.125
- vis_gain: float32 [2, 1024], replicated, may hold values from 0.5 to 2
- vis_bias: float32 [2, 1024], replicated, may hold values from -3 to 3
- v_qkv: bfloat16 [3, 1024, 1024], P(None, ('section', 'dp'), 'mp'), may hold values from -0.1875 to 0.1875
- v_out: bfloat16 [1024, 1024], P('mp', ('section', 'dp')), may hold values from -0.1875 to 0.1875
- v_up: bfloat16 [1024, 4096], P(('section', 'dp'), 'mp'), may hold values from -0.1875 to 0.1875
- v_down: bfloat16 [4096, 1024], P('mp', ('section', 'dp')), may hold values from -0.09375 to 0.09375
- v_proj: bfloat16 [4096, 4096], P(('section', 'dp'), 'mp'), may hold values from -0.09375 to 0.09375
Outputs:
- hidden: bfloat16 [4, 4096, 4096], P('section', ('dp', 'mp'))
- token_weight: float32 [4, 4096], P('section', ('dp', 'mp'))
Inputs may be any that keep to these rules, and one draw needn't show every extreme that they name: `tile_batch`: in every data-parallel index, the 2 tiles of each section index go 1 to each of two different micro-batches; one micro-batch receives 1 tiles from every section index. `tile_offset`: offsets are multiples of 64; the runs of one sequence never intersect. `loss_mask`: the first position of every sequence is a one.
All inputs are finite; a program needn't handle non-finite values.
Results may differ from a plain program's by a relative error of at most 0.025.
Values may be sent and summed in bfloat16 or wider, within the bound.
A program may use at most 192 MiB of HBM per device.

v0:
```python
import jax
import jax.numpy as jnp
from jax import lax
from jax.sharding import Mesh
from jax.sharding import PartitionSpec as P

HD = 128
VHD = 64
GRID = 16
PATCH = 256
POOL = 64
SECTION_DP = ("section", "dp_0", "dp_1")
SECTION_DP_MP = ("section", "dp_0", "dp_1", "mp")
DP = ("dp_0", "dp_1")
DP_MP = ("dp_0", "dp_1", "mp")
EPS = 1e-05
ROPE_BASE = 500000.0
BLOCKED = -1e30


def layer_norm(values, gain, bias):
    wide = values.astype(jnp.float32)
    center = wide - jnp.mean(wide, axis=-1, keepdims=True)
    spread = jnp.mean(center * center, axis=-1, keepdims=True)
    return (center * lax.rsqrt(spread + EPS) * gain + bias).astype(jnp.bfloat16)


def rms_norm(values, gain):
    wide = values.astype(jnp.float32)
    power = jnp.mean(wide * wide, axis=-1, keepdims=True)
    return (wide * lax.rsqrt(power + EPS) * gain).astype(jnp.bfloat16)


def pixel_shuffle(states):
    tile_count = states.shape[0] // PATCH
    side_half = GRID // 2
    width = states.shape[1]
    arranged = states.reshape(tile_count, side_half, 2, side_half, 2, width)
    return arranged.transpose(0, 1, 3, 2, 4, 5).reshape(
        tile_count * side_half * side_half, 4 * width
    )


def gathered(array, axis):
    copies = jnp.broadcast_to(array, (lax.axis_size(axis), *array.shape))
    return lax.all_to_all(copies, axis, split_axis=0, concat_axis=0, tiled=True)


def block_sum(partial_value):
    everything = gathered(partial_value.astype(jnp.bfloat16), "mp")
    return jnp.sum(everything.astype(jnp.float32), axis=0)


def transposed_dot(left, right):
    return lax.dot_general(
        left, right, (((1,), (1,)), ((), ())), preferred_element_type=jnp.float32
    )


def rope_tables(length):
    half_width = HD // 2
    freqs = ROPE_BASE ** (-2.0 * jnp.arange(half_width, dtype=jnp.float32) / HD)
    angles = jnp.arange(length, dtype=jnp.float32)[:, None] * freqs[None, :]
    cosine, sinus = (jnp.cos(angles), jnp.sin(angles))
    return (jnp.concatenate([cosine, cosine], axis=1), jnp.concatenate([-sinus, sinus], axis=1))


def encode_tiles(patches, vis_gain, vis_bias, small, proj_full):
    tile_count = patches.shape[0] // PATCH
    width = patches.shape[1]
    local = width // lax.axis_size("mp")
    head_count = local // VHD
    normed = layer_norm(patches, vis_gain[0], vis_bias[0])
    joined = jnp.dot(normed, small[:, : 3 * local], preferred_element_type=jnp.float32)
    joined = joined.astype(jnp.bfloat16).reshape(tile_count, PATCH, 3, head_count, VHD)
    query, keyed, valued = (joined[:, :, index] for index in range(3))
    scores = jnp.einsum("tqhd,tkhd->thqk", query, keyed, preferred_element_type=jnp.float32)
    probs = jax.nn.softmax(scores * VHD ** (-0.5), axis=-1).astype(jnp.bfloat16)
    mixed = jnp.einsum("thqk,tkhd->tqhd", probs, valued, preferred_element_type=jnp.float32)
    mixed = mixed.astype(jnp.bfloat16).reshape(tile_count * PATCH, local)
    attended = block_sum(transposed_dot(mixed, small[:, 3 * local : 4 * local]))
    residual = (patches.astype(jnp.float32) + attended).astype(jnp.bfloat16)
    normed_two = layer_norm(residual, vis_gain[1], vis_bias[1])
    hidden = small.shape[1] // 2 - 2 * local
    up = small[:, 4 * local : 4 * local + hidden]
    down = small[:, 4 * local + hidden :]
    inner = jax.nn.gelu(
        jnp.dot(normed_two, up, preferred_element_type=jnp.float32), approximate=False
    ).astype(jnp.bfloat16)
    fed = block_sum(transposed_dot(inner, down))
    states = (residual.astype(jnp.float32) + fed).astype(jnp.bfloat16)
    return jnp.dot(pixel_shuffle(states), proj_full, preferred_element_type=jnp.float32).astype(
        jnp.bfloat16
    )


def decoder_layer(state, allowed, cosine, sinus, w_joined, w_out):
    blocks = gathered(state, "mp")
    count, length, block_width = blocks.shape
    query_width = w_out.shape[0] // count
    rows = jnp.moveaxis(blocks, 0, 1).reshape(length, count * block_width)
    wide = rows.astype(jnp.float32)
    scale = lax.rsqrt(jnp.mean(wide * wide, axis=-1, keepdims=True) + EPS)
    joined = jnp.dot(rows, w_joined, preferred_element_type=jnp.float32) * scale
    heads = joined.reshape(length, joined.shape[1] // HD, HD)
    turned = heads * cosine[:, None] + jnp.roll(heads, HD // 2, axis=-1) * sinus[:, None]
    query_heads = query_width // HD
    query = turned[:, :query_heads].astype(jnp.bfloat16)
    keyed = turned[:, query_heads].astype(jnp.bfloat16)
    valued = heads[:, query_heads + 1].astype(jnp.bfloat16)
    scores = jnp.einsum("qgd,sd->gqs", query, keyed, preferred_element_type=jnp.float32)
    scores = jnp.where(allowed, scores * HD ** (-0.5), BLOCKED)
    probs = jax.nn.softmax(scores, axis=-1).astype(jnp.bfloat16)
    mixed = (
        jnp.einsum("gqs,sd->qgd", probs, valued, preferred_element_type=jnp.float32)
        .astype(jnp.bfloat16)
        .reshape(length, query_width)
    )
    parts = jnp.moveaxis(gathered(mixed, "mp"), 0, 1).reshape(length, count * query_width)
    added = jnp.dot(parts, w_out, preferred_element_type=jnp.float32)
    return (state.astype(jnp.float32) + added).astype(jnp.bfloat16)


def shards(
    text,
    patches,
    segments,
    loss_mask,
    tile_batch,
    tile_offset,
    attn_gain,
    w_query,
    w_kv,
    w_out,
    vis_gain,
    vis_bias,
    v_qkv,
    v_out,
    v_up,
    v_down,
    v_proj,
):
    sections = lax.axis_size("section")
    section_at = lax.axis_index("section")
    parts = lax.axis_size("mp")
    copies = lax.axis_size(DP)
    copy_at = lax.axis_index(DP)
    small = jnp.concatenate([v_qkv[0], v_qkv[1], v_qkv[2], v_out.T, v_up, v_down.T], axis=1)
    small = lax.all_gather(small, SECTION_DP, axis=0, tiled=True)
    proj_full = lax.all_gather(v_proj, SECTION_DP, axis=0, tiled=True)
    model_width = w_query.shape[1]
    row_share = model_width // copies
    pick = lambda array: lax.dynamic_slice_in_dim(array, copy_at * row_share, row_share, 0)
    own_rows = jnp.concatenate([pick(w_query[0]), pick(w_kv[0, 0]), pick(w_kv[0, 1])], axis=1)
    own_gain = lax.dynamic_slice_in_dim(attn_gain[0], copy_at * row_share, row_share, 0)
    own_rows = (own_rows.astype(jnp.float32) * own_gain[:, None]).astype(jnp.bfloat16)
    block_width = model_width // parts
    col_share = block_width // copies
    own_out = w_out[0].reshape(w_out.shape[1], parts, copies, col_share)
    own_out = lax.dynamic_slice_in_dim(own_out, copy_at, 1, 2)[:, :, 0]
    own_out = lax.all_to_all(
        jnp.moveaxis(own_out, 1, 0), "mp", split_axis=0, concat_axis=0, tiled=True
    )
    joined_all = lax.all_gather(own_rows, SECTION_DP).reshape(
        sections, model_width, own_rows.shape[1]
    )
    out_all = lax.all_gather(own_out, SECTION_DP).reshape(
        sections, copies, parts * w_out.shape[1], col_share
    )
    text_blocks = lax.all_to_all(
        jnp.moveaxis(text[0].reshape(text.shape[1], parts, block_width), 1, 0),
        "mp",
        split_axis=0,
        concat_axis=0,
        tiled=True,
    ).reshape(text.shape[1] * parts, block_width)
    embedded = encode_tiles(patches, vis_gain, vis_bias, small, proj_full)
    length = segments.shape[2]
    tiles_here = embedded.shape[0] // POOL
    batch_all = tile_batch[0]
    offset_all = tile_offset[0]
    own_batch = lax.dynamic_slice_in_dim(batch_all, section_at * tiles_here, tiles_here, 0)
    capacity = tiles_here // 2
    block_rows = capacity * POOL
    local_ids = jnp.arange(tiles_here, dtype=jnp.int32)
    local_same = (own_batch[:, None] == own_batch[None, :]) & (
        local_ids[None, :] < local_ids[:, None]
    )
    local_rank = jnp.sum(local_same.astype(jnp.int32), axis=1)
    send_rows = jnp.arange(sections * block_rows, dtype=jnp.int32)
    send_target = send_rows // block_rows
    send_rank = send_rows % block_rows // POOL
    send_match = (own_batch[None, :] == send_target[:, None]) & (
        local_rank[None, :] == send_rank[:, None]
    )
    own_rows = jnp.arange(tiles_here * POOL, dtype=jnp.int32)
    send_pick = jnp.repeat(send_match, POOL, axis=1) & (
        (own_rows % POOL)[None, :] == (send_rows % POOL)[:, None]
    )
    blocks = jnp.dot(
        send_pick.astype(jnp.bfloat16), embedded, preferred_element_type=jnp.float32
    ).astype(jnp.bfloat16)
    arrived = lax.all_to_all(blocks, "section", split_axis=0, concat_axis=0, tiled=True)
    tile_ids = jnp.arange(batch_all.shape[0], dtype=jnp.int32)
    source_ids = tile_ids // tiles_here
    tile_same = (
        (batch_all[:, None] == batch_all[None, :])
        & (source_ids[:, None] == source_ids[None, :])
        & (tile_ids[None, :] < tile_ids[:, None])
    )
    tile_rank = jnp.sum(tile_same.astype(jnp.int32), axis=1)
    slot_rows = jnp.arange(sections * block_rows, dtype=jnp.int32)
    slot_source = slot_rows // block_rows
    slot_rank = slot_rows % block_rows // POOL
    match = (
        (batch_all[None, :] == section_at)
        & (source_ids[None, :] == slot_source[:, None])
        & (tile_rank[None, :] == slot_rank[:, None])
    )
    slot_place = jnp.sum(match.astype(jnp.int32) * offset_all[None, :], axis=1) + slot_rows % POOL
    slot_valid = jnp.any(match, axis=1)
    places = jnp.arange(length, dtype=jnp.int32)
    picker = ((places[:, None] == slot_place[None, :]) & slot_valid[None, :]).astype(jnp.bfloat16)
    image_cols = jnp.dot(picker, arrived, preferred_element_type=jnp.float32).astype(jnp.bfloat16)
    covered = jnp.any(
        (batch_all[None, :] == section_at)
        & (places[:, None] >= offset_all[None, :])
        & (places[:, None] < offset_all[None, :] + POOL),
        axis=1,
    )
    state = jnp.where(covered[:, None], image_cols, text_blocks)
    segment_ids = segments[0, 0]
    allowed = (segment_ids[:, None] == segment_ids[None, :]) & (places[None, :] <= places[:, None])
    cosine, sinus = rope_tables(length)
    for layer in range(sections):
        w_layer = jnp.moveaxis(out_all[layer], 0, 1).reshape(out_all.shape[2], block_width)
        state = decoder_layer(state, allowed, cosine, sinus, joined_all[layer], w_layer)
    hidden = lax.all_to_all(
        state.reshape(parts, length // parts, block_width),
        "mp",
        split_axis=0,
        concat_axis=0,
        tiled=True,
    )
    hidden = jnp.moveaxis(hidden, 0, 1).reshape(length // parts, model_width)
    totals = lax.psum(jnp.sum(loss_mask), SECTION_DP_MP)
    scaling = float(sections * lax.axis_size(DP) * length)
    token_weight = loss_mask.astype(jnp.float32) * scaling / totals.astype(jnp.float32)
    return (hidden[None], token_weight)


def solution(mesh):
    split = Mesh(
        mesh.devices.reshape(mesh.shape["section"], 4, 2, mesh.shape["mp"]),
        ("section", "dp_0", "dp_1", "mp"),
    )
    return jax.shard_map(
        shards,
        mesh=split,
        in_specs=(
            P("section", DP_MP, None),
            P(SECTION_DP, None),
            P("section", DP, None),
            P("section", DP_MP),
            P(DP, None),
            P(DP, None),
            P("section", None),
            P("section", None, "mp"),
            P("section", None, None, "mp"),
            P("section", "mp", None),
            P(),
            P(),
            P(None, SECTION_DP, "mp"),
            P("mp", SECTION_DP),
            P(SECTION_DP, "mp"),
            P("mp", SECTION_DP),
            P(SECTION_DP, "mp"),
        ),
        out_specs=(P("section", DP_MP, None), P("section", DP_MP)),
        check_vma=False,
    )
```

profile of v0, /device:TPU:1, one launch (start us, length us, event | category | flops | bytes accessed | tf_op | source)
XLA Modules:
  0.0 700.2 jit_solution(4039534892102669239)
XLA Ops:
  13.3 1.7 fusion.220
  17.3 6.5 copy.169
  25.3 13.5 %all_to_all.77 = bf16[4,512,128]{2,1,0:T(8,128)(2,1)} all-to-all(bf16[4,512,128]{2,1,0:T(8,128)(2,1)S(1)} %bitcast.271), channel_id=1, replica_groups=mesh['section'=4,'dp_0'=4,'dp_1'=2,'mp'=4] {'mp'}, dimensions={0} | all-to-all | bytes 1048576 | tf_op jit(solution)/shard_map/all_to_all | solution.py:161
  39.5 25.9 %all-gather.6.cloned.1.call-done = bf16[1024,3072]{1,0:T(8,128)(2,1)} async-done(((bf16[32,3072]{1,0:T(8,128)(2,1)}), bf16[1024,3072]{1,0:T(8,128)(2,1)}) %all-gather.6.cloned.1.call-update) | async-done | bytes 6291472 | tf_op jit(solution)/shard_map/all_gather | solution.py:149
  65.4 2.5 fusion.67
  68.8 1.5 fusion.225
  73.1 2.1 fusion.228
  75.3 2.0 fusion.75
  79.7 52.3 %all_to_all.78 = bf16[4,512,1024]{2,1,0:T(8,128)(2,1)S(1)} all-to-all(bf16[4,512,1024]{2,1,0:T(8,128)(2,1)S(1)} %broadcast_in_dim.44), channel_id=1, replica_groups=mesh['section'=4,'dp_0'=4,'dp_1'=2,'mp'=4] {'mp'}, dimensions={0} | all-to-all | bytes 8388608 | tf_op jit(solution)/shard_map/all_to_all | solution.py:46
  133.7 8.5 %fusion.64 = bf16[512,1024]{1,0:T(8,128)(2,1)S(1)} fusion(bf16[1024,3072]{1,0:T(8,128)(2,1)} %all-gather.6.cloned.1.call-done, bf16[512,1024]{1,0:T(8,128)(2,1)S(1)} %get-tuple-element.3, f32[1024]{0:T(1024)S(1)} %bitcast.283, f32[1024]{0:T(1024)S(1)} %bitcast.282, f32[512]{0:T(512)S(1)} %add_rsqrt_fusion.4, f32[512]{0:T(512)S(1)} %broadcast_multiply_fusion), kind=kOutput, calls=%fused_computation.109 | convolution fusion | flops 2185232384 | bytes 6303744 | tf_op jit(solution)/shard_map/dot_general | solution.py:55
  142.2 2.5 broadcast_in_dim.45
  144.7 5.0 all-to-all-start.1
  152.6 44.7 %all-to-all-done.1 = bf16[4,512,1024]{2,1,0:T(8,128)(2,1)} async-done(((bf16[4,512,1024]{2,1,0:T(8,128)(2,1)}), bf16[4,512,1024]{2,1,0:T(8,128)(2,1)}, u32[]{:S(2)}, u32[]{:S(2)}) %all-to-all-start.1) | async-done | bytes 4194336 | tf_op jit(solution)/shard_map/all_to_all | solution.py:46
  197.3 4.5 all-to-all-start.3
  201.8 3.7 convert_reduce_fusion
  208.0 5.7 convolution_convert_fusion.2
  214.7 3.5 all-to-all-start.2
  218.4 6.7 all-to-all-done.2
  225.1 1.8 fusion.70
  227.4 2.2 broadcast_in_dim.46
  229.7 5.3 all-to-all-start.4
  236.5 43.3 %all-to-all-done.4 = bf16[4,512,1024]{1,2,0:T(8,128)(2,1)} async-done(((bf16[4,512,1024]{1,2,0:T(8,128)(2,1)}), bf16[4,512,1024]{1,2,0:T(8,128)(2,1)}, u32[]{:S(2)}, u32[]{:S(2)}) %all-to-all-start.4) | async-done | bytes 4194336 | tf_op jit(solution)/shard_map/all_to_all | solution.py:46
  279.7 3.1 multiply_reduce_fusion.3
  282.9 16.0 %fusion.218 = (bf16[8,512,768]{2,1,0:T(8,128)(2,1)}, bf16[8,512,768]{2,1,0:T(8,128)(2,1)}, bf16[8,512,768]{2,1,0:T(8,128)(2,1)}, bf16[8,512,768]{2,1,0:T(8,128)(2,1)S(1)}) fusion(bf16[32,512,768]{2,1,0:T(8,128)(2,1)} %all-gather.10.cloned.1.call-done), kind=kLoop, calls=%fused_computation.300 | loop fusion | bytes 50331648 | tf_op jit(solution)/shard_map/slice | solution.py:237
  298.9 5.3 convolution_multiply_fusion.3
  304.2 1.6 copy.164
  305.8 1.9 copy.165
  309.5 2.1 fusion.233
  314.5 4.4 all-to-all-start.5
  319.0 12.2 %fusion.219 = (bf16[32,512,128]{2,1,0:T(8,128)(2,1)}, bf16[32,512,128]{2,1,0:T(8,128)(2,1)}, bf16[32,512,128]{2,1,0:T(8,128)(2,1)}, bf16[32,512,128]{2,1,0:T(8,128)(2,1)}) fusion(bf16[128,512,128]{2,1,0:T(8,128)(2,1)} %all-gather.12.cloned.1.call-done), kind=kLoop, calls=%fused_computation.301 | loop fusion | bytes 33554432 | tf_op jit(solution)/shard_map/slice | solution.py:236
  331.2 6.5 copy.171
  337.7 2.7 all-to-all-done.5
  340.4 6.2 add_convert_fusion.3
  348.4 45.9 %all_to_all.79 = bf16[4,512,1024]{1,2,0:T(8,128)(2,1)S(1)} all-to-all(bf16[4,512,1024]{1,2,0:T(8,128)(2,1)S(1)} %broadcast_in_dim.52), channel_id=1, replica_groups=mesh['section'=4,'dp_0'=4,'dp_1'=2,'mp'=4] {'mp'}, dimensions={0} | all-to-all | bytes 8388608 | tf_op jit(solution)/shard_map/all_to_all | solution.py:46
  395.3 3.5 convolution_multiply_fusion.2
  398.8 1.7 copy.173
  400.5 1.9 copy.174
  404.1 2.1 fusion.234
  409.2 4.4 all-to-all-start.8
  413.6 6.6 copy.178
  420.2 12.8 %all-to-all-done.8 = bf16[4,512,512]{1,2,0:T(8,128)(2,1)} async-done(((bf16[4,512,512]{1,2,0:T(8,128)(2,1)}), bf16[4,512,512]{1,2,0:T(8,128)(2,1)}, u32[]{:S(2)}, u32[]{:S(2)}) %all-to-all-start.8) | async-done | bytes 2097184 | tf_op jit(solution)/shard_map/all_to_all | solution.py:46
  433.0 5.2 add_convert_fusion.2
  439.2 43.9 %all_to_all.80 = bf16[4,512,1024]{1,2,0:T(8,128)(2,1)S(1)} all-to-all(bf16[4,512,1024]{1,2,0:T(8,128)(2,1)S(1)} %broadcast_in_dim.54), channel_id=1, replica_groups=mesh['section'=4,'dp_0'=4,'dp_1'=2,'mp'=4] {'mp'}, dimensions={0} | all-to-all | bytes 8388608 | tf_op jit(solution)/shard_map/all_to_all | solution.py:46
  484.1 3.5 convolution_multiply_fusion.1
  487.6 1.7 copy.180
  489.3 1.9 copy.181
  493.0 2.1 fusion.235
  498.0 4.5 all-to-all-start.10
  502.5 6.6 copy.185
  509.1 10.8 %all-to-all-done.10 = bf16[4,512,512]{1,2,0:T(8,128)(2,1)} async-done(((bf16[4,512,512]{1,2,0:T(8,128)(2,1)}), bf16[4,512,512]{1,2,0:T(8,128)(2,1)}, u32[]{:S(2)}, u32[]{:S(2)}) %all-to-all-start.10) | async-done | bytes 2097184 | tf_op jit(solution)/shard_map/all_to_all | solution.py:46
  519.9 5.2 add_convert_fusion.1
  526.0 41.8 %all_to_all.81 = bf16[4,512,1024]{1,2,0:T(8,128)(2,1)S(1)} all-to-all(bf16[4,512,1024]{1,2,0:T(8,128)(2,1)S(1)} %broadcast_in_dim.56), channel_id=1, replica_groups=mesh['section'=4,'dp_0'=4,'dp_1'=2,'mp'=4] {'mp'}, dimensions={0} | all-to-all | bytes 8388608 | tf_op jit(solution)/shard_map/all_to_all | solution.py:46
  568.7 3.5 convolution_multiply_fusion
  572.3 1.6 copy.187
  573.9 1.9 copy.188
  577.5 2.1 fusion.236
  581.1 1.6 broadcast_in_dim.57
  582.7 3.6 all-to-all-start.12
  586.3 6.5 copy.192
  592.8 8.8 %all-to-all-done.12 = bf16[4,512,512]{1,2,0:T(8,128)(2,1)S(1)} async-done(((bf16[4,512,512]{1,2,0:T(8,128)(2,1)}), bf16[4,512,512]{1,2,0:T(8,128)(2,1)S(1)}, u32[]{:S(2)}, u32[]{:S(2)}) %all-to-all-start.12) | async-done | bytes 2097184 | tf_op jit(solution)/shard_map/all_to_all | solution.py:46
  601.6 5.5 add_convert_fusion
  607.1 3.6 all-to-all-start.13
  611.4 78.2 %psum.7 = s32[]{:T(128)} all-reduce(s32[]{:T(128)} %reduce_sum.189), channel_id=1, replica_groups=mesh['section'=4,'dp_0'=4,'dp_1'=2,'mp'=4] {'section','dp_0','dp_1','mp'}, use_global_device_ids=true, to_apply=%region_26.27 | all-reduce | flops 1 | bytes 8 | tf_op jit(solution)/shard_map/psum | solution.py:246
  691.6 1.6 broadcast_in_dim_reshape.3
  (148 shorter events, 52.3 us)
Async XLA Ops:
  7.2 6.1 copy-start
  7.2 58.2 %all-gather.6.cloned.1.call-start = ((), (), s32[]{:S(2)}) async-start(), calls=%async_computation.14 | async-start | bytes 6488064 | tf_op jit(solution)/shard_map/all_gather | solution.py:149
  11.8 0.7 copy-start.7
  12.5 195.5 %all-gather.8.cloned.1.call-start = ((), (), s32[]{:S(2)}) async-start(), calls=%async_computation.15 | async-start | bytes 8650752 | tf_op jit(solution)/shard_map/all_gather | solution.py:150
  13.2 269.6 %all-gather.10.cloned.1.call-start = ((), (), s32[]{:S(2)}) async-start(), calls=%async_computation.16 | async-start | bytes 25952256 | tf_op jit(solution)/shard_map/all_gather | solution.py:164
  17.3 301.7 %all-gather.12.cloned.1.call-start = ((), (), s32[]{:S(2)}) async-start(), calls=%async_computation.17 | async-start | bytes 17301504 | tf_op jit(solution)/shard_map/all_gather | solution.py:167
  23.8 15.0 %copy-start.2 = (bf16[512,1024]{1,0:T(8,128)(2,1)S(1)}, bf16[512,1024]{1,0:T(8,128)(2,1)}, u32[]{:S(2)}) copy-start(bf16[512,1024]{1,0:T(8,128)(2,1)} %param.18) | copy-start | bytes 3145732
  25.2 14.2 %copy-start.9 = (f32[2,1024]{1,0:T(2,128)S(1)}, f32[2,1024]{1,0:T(2,128)}, u32[]{:S(2)}) copy-start(f32[2,1024]{1,0:T(2,128)} %param.27) | copy-start | bytes 24580
  25.3 14.2 %copy-start.10 = (f32[2,1024]{1,0:T(2,128)S(1)}, f32[2,1024]{1,0:T(2,128)}, u32[]{:S(2)}) copy-start(f32[2,1024]{1,0:T(2,128)} %param.28) | copy-start | bytes 24580
  144.7 5.0 copy-start.3
  144.7 52.5 %all-to-all-start.1 = ((bf16[4,512,1024]{2,1,0:T(8,128)(2,1)}), bf16[4,512,1024]{2,1,0:T(8,128)(2,1)}, u32[]{:S(2)}, u32[]{:S(2)}) async-start(bf16[4,512,1024]{2,1,0:T(8,128)(2,1)} %broadcast_in_dim.45), calls=%async_computation.1 | async-start | bytes 8388608 | tf_op jit(solution)/shard_map/all_to_all | solution.py:46
  149.7 2.1 copy-start.11
  149.7 2.8 copy-start.12
  197.3 17.5 %all-to-all-start.3 = ((bf16[4,128,1024]{2,1,0:T(8,128)(2,1)}), bf16[4,128,1024]{2,1,0:T(8,128)(2,1)}, u32[]{:S(2)}, u32[]{:S(2)}) async-start(bf16[4,128,1024]{2,1,0:T(8,128)(2,1)} %bitcast.236), calls=%async_computation.3 | async-start | bytes 2097152 | tf_op jit(solution)/shard_map/all_to_all | solution.py:170
  214.7 10.4 %all-to-all-start.2 = ((bf16[4,64,1024]{2,1,0:T(8,128)(2,1)}), bf16[4,64,1024]{2,1,0:T(8,128)(2,1)S(1)}, u32[]{:S(2)}, u32[]{:S(2)}) async-start(bf16[4,64,1024]{2,1,0:T(8,128)(2,1)} %bitcast.20), calls=%async_computation.2 | async-start | bytes 1048576 | tf_op jit(solution)/shard_map/all_to_all | solution.py:203
  229.7 50.0 %all-to-all-start.4 = ((bf16[4,512,1024]{1,2,0:T(8,128)(2,1)}), bf16[4,512,1024]{1,2,0:T(8,128)(2,1)}, u32[]{:S(2)}, u32[]{:S(2)}) async-start(bf16[4,512,1024]{1,2,0:T(8,128)(2,1)} %broadcast_in_dim.46), calls=%async_computation.4 | async-start | bytes 8388608 | tf_op jit(solution)/shard_map/all_to_all | solution.py:46
  235.0 1.2 copy-start.8
  314.5 25.8 %all-to-all-start.5 = ((bf16[4,512,512]{1,2,0:T(8,128)(2,1)}), bf16[4,512,512]{1,2,0:T(8,128)(2,1)}, u32[]{:S(2)}, u32[]{:S(2)}) async-start(bf16[4,512,512]{1,2,0:T(8,128)(2,1)} %broadcast_in_dim.49), calls=%async_computation.5 | async-start | bytes 4194304 | tf_op jit(solution)/shard_map/all_to_all | solution.py:46
  348.1 47.2 %slice-start.4 = ((s8[6291456]{0:T(1024)(128)(4,1)}), s8[4194304]{0:T(1024)(128)(4,1)S(1)}, s32[]{:S(2)}) async-start(s8[6291456]{0:T(1024)(128)(4,1)} %bitcast.251), calls=%async_computation.22 | async-start | bytes 8388608
  348.4 46.9 %slice-start.5 = ((s8[6291456]{0:T(1024)(128)(4,1)}), s8[2097152]{0:T(1024)(128)(4,1)S(1)}, s32[]{:S(2)}) async-start(s8[6291456]{0:T(1024)(128)(4,1)} %bitcast.251), calls=%async_computation.23 | async-start | bytes 4194304
  409.2 23.8 %all-to-all-start.8 = ((bf16[4,512,512]{1,2,0:T(8,128)(2,1)}), bf16[4,512,512]{1,2,0:T(8,128)(2,1)}, u32[]{:S(2)}, u32[]{:S(2)}) async-start(bf16[4,512,512]{1,2,0:T(8,128)(2,1)} %broadcast_in_dim.53), calls=%async_computation.8 | async-start | bytes 4194304 | tf_op jit(solution)/shard_map/all_to_all | solution.py:46
  413.6 19.4 %copy-start.4 = (bf16[512,1024]{1,0:T(8,128)(2,1)S(1)}, bf16[512,1024]{1,0:T(8,128)(2,1)}, u32[]{:S(2)}) copy-start(bf16[512,1024]{1,0:T(8,128)(2,1)} %add_convert_fusion.3) | copy-start | bytes 3145732
  438.2 1.0 copy-start.5
  438.8 45.3 %slice-start.2 = ((s8[6291456]{0:T(1024)(128)(4,1)}), s8[4194304]{0:T(1024)(128)(4,1)S(1)}, s32[]{:S(2)}) async-start(s8[6291456]{0:T(1024)(128)(4,1)} %bitcast.248), calls=%async_computation.20 | async-start | bytes 8388608
  439.2 44.9 %slice-start.3 = ((s8[6291456]{0:T(1024)(128)(4,1)}), s8[2097152]{0:T(1024)(128)(4,1)S(1)}, s32[]{:S(2)}) async-start(s8[6291456]{0:T(1024)(128)(4,1)} %bitcast.248), calls=%async_computation.21 | async-start | bytes 4194304
  498.0 21.8 %all-to-all-start.10 = ((bf16[4,512,512]{1,2,0:T(8,128)(2,1)}), bf16[4,512,512]{1,2,0:T(8,128)(2,1)}, u32[]{:S(2)}, u32[]{:S(2)}) async-start(bf16[4,512,512]{1,2,0:T(8,128)(2,1)} %broadcast_in_dim.55), calls=%async_computation.10 | async-start | bytes 4194304 | tf_op jit(solution)/shard_map/all_to_all | solution.py:46
  502.5 17.4 %copy-start.6 = (bf16[512,1024]{1,0:T(8,128)(2,1)S(1)}, bf16[512,1024]{1,0:T(8,128)(2,1)}, u32[]{:S(2)}) copy-start(bf16[512,1024]{1,0:T(8,128)(2,1)} %copy-done.5) | copy-start | bytes 3145732
  525.6 43.1 %slice-start = ((s8[6291456]{0:T(1024)(128)(4,1)}), s8[4194304]{0:T(1024)(128)(4,1)S(1)}, s32[]{:S(2)}) async-start(s8[6291456]{0:T(1024)(128)(4,1)} %bitcast.245), calls=%async_computation.18 | async-start | bytes 8388608
  526.0 42.8 %slice-start.1 = ((s8[6291456]{0:T(1024)(128)(4,1)}), s8[2097152]{0:T(1024)(128)(4,1)S(1)}, s32[]{:S(2)}) async-start(s8[6291456]{0:T(1024)(128)(4,1)} %bitcast.245), calls=%async_computation.19 | async-start | bytes 4194304
  582.7 18.9 %all-to-all-start.12 = ((bf16[4,512,512]{1,2,0:T(8,128)(2,1)}), bf16[4,512,512]{1,2,0:T(8,128)(2,1)S(1)}, u32[]{:S(2)}, u32[]{:S(2)}) async-start(bf16[4,512,512]{1,2,0:T(8,128)(2,1)} %broadcast_in_dim.57), calls=%async_computation.12 | async-start | bytes 4194304 | tf_op jit(solution)/shard_map/all_to_all | solution.py:46
  607.1 3.7 copy-start.13
  607.1 83.7 %all-to-all-start.13 = ((bf16[4,128,1024]{2,1,0:T(8,128)(2,1)}), bf16[4,128,1024]{2,1,0:T(8,128)(2,1)S(1)}, u32[]{:S(2)}, u32[]{:S(2)}) async-start(bf16[4,128,1024]{2,1,0:T(8,128)(2,1)} %bitcast.273), calls=%async_computation.13 | async-start | bytes 2097152 | tf_op jit(solution)/shard_map/all_to_all | solution.py:238
  690.8 2.4 copy-start.1
Sparse Core Ops, SparseCore 0:
  12.6 52.7 all-gather.5
  67.7 51.5 all-gather.7
  121.5 91.5 all-gather.9
  215.2 71.9 all-gather.11
where the time goes:
time: 708 us; the launch traced here: 700 us
  blocking collectives  276 us (39%)
  waiting for transfers between devices  157 us (22%)
  local copies, waits for them, and re-layouts  114 us (16%)
  matrix products  70.6 us (10%)
  starting transfers between devices  39.1 us (6%)
  other arithmetic  27.5 us (4%)
  between operations  15.7 us (2%)
    all_to_all x4, blocking collectives, gathered(): return lax.all_to_all(copies, axis, split_axis=0, concat_axis=0, tiled=True)  184 us
    all_to_all x6, waiting for transfers between devices, gathered(): return lax.all_to_all(copies, axis, split_axis=0, concat_axis=0, tiled=True)  123 us
    psum x1, blocking collectives, shards(): totals = lax.psum(jnp.sum(loss_mask), SECTION_DP_MP)  78.2 us
    all_to_all x6, starting transfers between devices, gathered(): return lax.all_to_all(copies, axis, split_axis=0, concat_axis=0, tiled=True)  27.3 us
    transpose x4, local copies, waits for them, and re-layouts, shards(): jnp.moveaxis(out_all[layer], 0, 1).reshape(out_all.shape[2], block_width)  26.2 us
    all_gather x1, waiting for transfers between devices, shards(): small = lax.all_gather(small, SECTION_DP, axis=0, tiled=True)  25.9 us
    dot_general x4, matrix products, decoder_layer(): added = jnp.dot(parts, w_out, preferred_element_type=jnp.float32)  22.1 us
    slice x1, local copies, waits for them, and re-layouts, shards(): joined_all[layer]  16 us
  transfers between devices with their start and end apart: 13, of which 9 were waited for; matrix products, arithmetic and copies ran while one was open for 19% of the time, Pallas kernels for 0%

commit v1 on v0

--- a/solution.py
+++ b/solution.py
@@ -146,7 +146,9 @@
     copies = lax.axis_size(DP)
     copy_at = lax.axis_index(DP)
     small = jnp.concatenate([v_qkv[0], v_qkv[1], v_qkv[2], v_out.T, v_up, v_down.T], axis=1)
-    small = lax.all_gather(small, SECTION_DP, axis=0, tiled=True)
+    small = jnp.concatenate(
+        lax.all_to_all(jnp.stack([small] * lax.axis_size(SECTION_DP)), SECTION_DP, 0, 0), axis=0
+    )
     proj_full = lax.all_gather(v_proj, SECTION_DP, axis=0, tiled=True)
     model_width = w_query.shape[1]
     row_share = model_width // copies

time: 708 us -> 808 us (1.14)
  waiting for transfers between devices: 157 us -> 212 us
  blocking collectives: 276 us -> 305 us
  starting transfers between devices: 39.1 us -> 56.2 us
    all_to_all x0 -> x1, waiting for transfers between devices: none -> 86.5 us  [shards(): lax.all_to_all(jnp.stack([small] * lax.axis_size(SECTION_DP)), SECTION_DP...]
    psum x1, blocking collectives: 78.2 us -> 117 us  [shards(): totals = lax.psum(jnp.sum(loss_mask), SECTION_DP_MP)]
    all_gather x1 -> x0, waiting for transfers between devices: 25.9 us -> none  [shards(): small = lax.all_gather(small, SECTION_DP, axis=0, tiled=True)]
    all_to_all x6, waiting for transfers between devices: 123 us -> 111 us  [gathered(): return lax.all_to_all(copies, axis, split_axis=0, concat_axis=0, tiled=True)]
    all_to_all x0 -> x1, starting transfers between devices: none -> 10.1 us  [shards(): lax.all_to_all(jnp.stack([small] * lax.axis_size(SECTION_DP)), SECTION_DP...]
    all_to_all x4, blocking collectives: 184 us -> 175 us  [gathered(): return lax.all_to_all(copies, axis, split_axis=0, concat_axis=0, tiled=True)]
  transfers between devices with their start and end apart: 13 -> 13, of which waited for: 9 -> 8; matrix products, arithmetic and copies ran while one was open for 19% -> 17% of each run, Pallas kernels for 0% -> 0%
where the time goes in v1:
time: 808 us; the launch traced here: 800 us
  blocking collectives  305 us (38%)
  waiting for transfers between devices  212 us (26%)
  local copies, waits for them, and re-layouts  112 us (14%)
  matrix products  70.6 us (9%)
  starting transfers between devices  56.2 us (7%)
  other arithmetic  27.3 us (3%)
  between operations  15.8 us (2%)
    all_to_all x4, blocking collectives, gathered(): return lax.all_to_all(copies, axis, split_axis=0, concat_axis=0, tiled=True)  175 us
    psum x1, blocking collectives, shards(): totals = lax.psum(jnp.sum(loss_mask), SECTION_DP_MP)  117 us
    all_to_all x6, waiting for transfers between devices, gathered(): return lax.all_to_all(copies, axis, split_axis=0, concat_axis=0, tiled=True)  111 us
    all_to_all x1, waiting for transfers between devices, shards(): lax.all_to_all(jnp.stack([small] * lax.axis_size(SECTION_DP)), SECTION_DP...  86.5 us
    all_to_all x6, starting transfers between devices, gathered(): return lax.all_to_all(copies, axis, split_axis=0, concat_axis=0, tiled=True)  27.5 us
    transpose x4, local copies, waits for them, and re-layouts, shards(): jnp.moveaxis(out_all[layer], 0, 1).reshape(out_all.shape[2], block_width)  26.2 us
    dot_general x4, matrix products, decoder_layer(): added = jnp.dot(parts, w_out, preferred_element_type=jnp.float32)  22.1 us
  transfers between devices with their start and end apart: 13, of which 8 were waited for; matrix products, arithmetic and copies ran while one was open for 17% of the time, Pallas kernels for 0%

profile of v1, /device:TPU:1, one launch (start us, length us, event | category | flops | bytes accessed | tf_op | source)
XLA Modules:
  0.0 799.7 jit_solution(15561746464296306015)
XLA Ops:
  8.0 1.7 fusion.220
  12.0 6.5 copy.169
  19.9 13.4 %all_to_all.82 = bf16[4,512,128]{2,1,0:T(8,128)(2,1)} all-to-all(bf16[4,512,128]{2,1,0:T(8,128)(2,1)S(1)} %bitcast.272), channel_id=1, replica_groups=mesh['section'=4,'dp_0'=4,'dp_1'=2,'mp'=4] {'mp'}, dimensions={0} | all-to-all | bytes 1048576 | tf_op jit(solution)/shard_map/all_to_all | solution.py:163
  33.4 3.4 stack.2
  36.8 10.1 %all-to-all-start = ((bf16[32,32,3072]{2,1,0:T(8,128)(2,1)}), bf16[32,32,3072]{2,1,0:T(8,128)(2,1)}, u32[]{:S(2)}, u32[]{:S(2)}) async-start(bf16[32,32,3072]{2,1,0:T(8,128)(2,1)} %stack.2), calls=%async_computation | async-start | bytes 12582912 | tf_op jit(solution)/shard_map/all_to_all | solution.py:150
  47.6 86.5 %all-to-all-done = bf16[32,32,3072]{2,1,0:T(8,128)(2,1)} async-done(((bf16[32,32,3072]{2,1,0:T(8,128)(2,1)}), bf16[32,32,3072]{2,1,0:T(8,128)(2,1)}, u32[]{:S(2)}, u32[]{:S(2)}) %all-to-all-start) | async-done | bytes 6291488 | tf_op jit(solution)/shard_map/all_to_all | solution.py:150
  134.1 2.5 fusion.67
  141.8 2.1 fusion.228
  143.9 2.1 fusion.75
  146.4 1.6 convolution_convert_fusion.1
  148.5 47.1 %all_to_all.83 = bf16[4,512,1024]{2,1,0:T(8,128)(2,1)S(1)} all-to-all(bf16[4,512,1024]{2,1,0:T(8,128)(2,1)S(1)} %broadcast_in_dim.44), channel_id=1, replica_groups=mesh['section'=4,'dp_0'=4,'dp_1'=2,'mp'=4] {'mp'}, dimensions={0} | all-to-all | bytes 8388608 | tf_op jit(solution)/shard_map/all_to_all | solution.py:46
  197.4 8.6 %fusion.64 = bf16[512,1024]{1,0:T(8,128)(2,1)S(1)} fusion(bf16[1024,3072]{1,0:T(8,128)(2,1)} %bitcast.13, bf16[512,1024]{1,0:T(8,128)(2,1)S(1)} %get-tuple-element.3, f32[1024]{0:T(1024)S(1)} %bitcast.284, f32[1024]{0:T(1024)S(1)} %bitcast.283, f32[512]{0:T(512)S(1)} %add_rsqrt_fusion.4, f32[512]{0:T(512)S(1)} %broadcast_multiply_fusion), kind=kOutput, calls=%fused_computation.109 | convolution fusion | flops 2185232384 | bytes 6303744 | tf_op jit(solution)/shard_map/dot_general | solution.py:55
  205.9 2.5 broadcast_in_dim.45
  208.4 5.0 all-to-all-start.2
  216.3 38.8 %all-to-all-done.2 = bf16[4,512,1024]{2,1,0:T(8,128)(2,1)} async-done(((bf16[4,512,1024]{2,1,0:T(8,128)(2,1)}), bf16[4,512,1024]{2,1,0:T(8,128)(2,1)}, u32[]{:S(2)}, u32[]{:S(2)}) %all-to-all-start.2) | async-done | bytes 4194336 | tf_op jit(solution)/shard_map/all_to_all | solution.py:46
  255.1 4.5 all-to-all-start.4
  259.6 3.4 convert_reduce_fusion
  265.7 5.6 convolution_convert_fusion.2
  271.3 10.4 %all-to-all-start.3 = ((bf16[4,64,1024]{2,1,0:T(8,128)(2,1)}), bf16[4,64,1024]{2,1,0:T(8,128)(2,1)S(1)}, u32[]{:S(2)}, u32[]{:S(2)}) async-start(bf16[4,64,1024]{2,1,0:T(8,128)(2,1)} %bitcast.21), calls=%async_computation.3 | async-start | bytes 1048576 | tf_op jit(solution)/shard_map/all_to_all | solution.py:205
  281.9 13.7 %all-to-all-done.3 = bf16[4,64,1024]{2,1,0:T(8,128)(2,1)S(1)} async-done(((bf16[4,64,1024]{2,1,0:T(8,128)(2,1)}), bf16[4,64,1024]{2,1,0:T(8,128)(2,1)S(1)}, u32[]{:S(2)}, u32[]{:S(2)}) %all-to-all-start.3) | async-done | bytes 524320 | tf_op jit(solution)/shard_map/all_to_all | solution.py:205
  295.6 1.7 fusion.70
  297.8 2.2 broadcast_in_dim.46
  300.1 5.5 all-to-all-start.5
  307.0 42.0 %all-to-all-done.5 = bf16[4,512,1024]{1,2,0:T(8,128)(2,1)} async-done(((bf16[4,512,1024]{1,2,0:T(8,128)(2,1)}), bf16[4,512,1024]{1,2,0:T(8,128)(2,1)}, u32[]{:S(2)}, u32[]{:S(2)}) %all-to-all-start.5) | async-done | bytes 4194336 | tf_op jit(solution)/shard_map/all_to_all | solution.py:46
  349.0 3.1 multiply_reduce_fusion.3
  352.1 15.8 %fusion.218 = (bf16[8,512,768]{2,1,0:T(8,128)(2,1)}, bf16[8,512,768]{2,1,0:T(8,128)(2,1)}, bf16[8,512,768]{2,1,0:T(8,128)(2,1)}, bf16[8,512,768]{2,1,0:T(8,128)(2,1)S(1)}) fusion(bf16[32,512,768]{2,1,0:T(8,128)(2,1)} %all-gather.7.cloned.1.call-done), kind=kLoop, calls=%fused_computation.300 | loop fusion | bytes 50331648 | tf_op jit(solution)/shard_map/slice | solution.py:239
  368.0 5.3 convolution_multiply_fusion.3
  373.3 1.6 copy.164
  374.9 1.9 copy.165
  378.5 2.1 fusion.233
  383.6 4.4 all-to-all-start.6
  388.1 12.2 %fusion.219 = (bf16[32,512,128]{2,1,0:T(8,128)(2,1)}, bf16[32,512,128]{2,1,0:T(8,128)(2,1)}, bf16[32,512,128]{2,1,0:T(8,128)(2,1)}, bf16[32,512,128]{2,1,0:T(8,128)(2,1)}) fusion(bf16[128,512,128]{2,1,0:T(8,128)(2,1)} %all-gather.9.cloned.1.call-done), kind=kLoop, calls=%fused_computation.301 | loop fusion | bytes 33554432 | tf_op jit(solution)/shard_map/slice | solution.py:238
  400.3 6.5 copy.171
  407.9 6.2 add_convert_fusion.3
  415.9 44.9 %all_to_all.84 = bf16[4,512,1024]{1,2,0:T(8,128)(2,1)S(1)} all-to-all(bf16[4,512,1024]{1,2,0:T(8,128)(2,1)S(1)} %broadcast_in_dim.52), channel_id=1, replica_groups=mesh['section'=4,'dp_0'=4,'dp_1'=2,'mp'=4] {'mp'}, dimensions={0} | all-to-all | bytes 8388608 | tf_op jit(solution)/shard_map/all_to_all | solution.py:46
  461.8 3.5 convolution_multiply_fusion.2
  465.3 1.7 copy.173
  467.0 1.9 copy.174
  470.6 2.1 fusion.234
  475.6 4.4 all-to-all-start.9
  480.1 6.6 copy.178
  486.7 11.4 %all-to-all-done.9 = bf16[4,512,512]{1,2,0:T(8,128)(2,1)} async-done(((bf16[4,512,512]{1,2,0:T(8,128)(2,1)}), bf16[4,512,512]{1,2,0:T(8,128)(2,1)}, u32[]{:S(2)}, u32[]{:S(2)}) %all-to-all-start.9) | async-done | bytes 2097184 | tf_op jit(solution)/shard_map/all_to_all | solution.py:46
  498.1 5.2 add_convert_fusion.2
  504.3 42.5 %all_to_all.85 = bf16[4,512,1024]{1,2,0:T(8,128)(2,1)S(1)} all-to-all(bf16[4,512,1024]{1,2,0:T(8,128)(2,1)S(1)} %broadcast_in_dim.54), channel_id=1, replica_groups=mesh['section'=4,'dp_0'=4,'dp_1'=2,'mp'=4] {'mp'}, dimensions={0} | all-to-all | bytes 8388608 | tf_op jit(solution)/shard_map/all_to_all | solution.py:46
  547.7 3.5 convolution_multiply_fusion.1
  551.3 1.7 copy.180
  553.0 1.9 copy.181
  556.6 2.1 fusion.235
  561.7 4.5 all-to-all-start.11
  566.1 6.6 copy.185
  572.7 9.4 %all-to-all-done.11 = bf16[4,512,512]{1,2,0:T(8,128)(2,1)} async-done(((bf16[4,512,512]{1,2,0:T(8,128)(2,1)}), bf16[4,512,512]{1,2,0:T(8,128)(2,1)}, u32[]{:S(2)}, u32[]{:S(2)}) %all-to-all-start.11) | async-done | bytes 2097184 | tf_op jit(solution)/shard_map/all_to_all | solution.py:46
  582.1 5.2 add_convert_fusion.1
  588.2 40.4 %all_to_all.86 = bf16[4,512,1024]{1,2,0:T(8,128)(2,1)S(1)} all-to-all(bf16[4,512,1024]{1,2,0:T(8,128)(2,1)S(1)} %broadcast_in_dim.56), channel_id=1, replica_groups=mesh['section'=4,'dp_0'=4,'dp_1'=2,'mp'=4] {'mp'}, dimensions={0} | all-to-all | bytes 8388608 | tf_op jit(solution)/shard_map/all_to_all | solution.py:46
  629.6 3.5 convolution_multiply_fusion
  633.1 1.6 copy.187
  634.7 1.9 copy.188
  638.4 2.1 fusion.236
  643.5 3.6 all-to-all-start.13
  647.1 6.5 copy.192
  653.6 8.8 %all-to-all-done.13 = bf16[4,512,512]{1,2,0:T(8,128)(2,1)S(1)} async-done(((bf16[4,512,512]{1,2,0:T(8,128)(2,1)}), bf16[4,512,512]{1,2,0:T(8,128)(2,1)S(1)}, u32[]{:S(2)}, u32[]{:S(2)}) %all-to-all-start.13) | async-done | bytes 2097184 | tf_op jit(solution)/shard_map/all_to_all | solution.py:46
  662.4 5.5 add_convert_fusion
  668.0 3.6 all-to-all-start.14
  672.3 116.9 %psum.7 = s32[]{:T(128)} all-reduce(s32[]{:T(128)} %reduce_sum.189), channel_id=1, replica_groups=mesh['section'=4,'dp_0'=4,'dp_1'=2,'mp'=4] {'section','dp_0','dp_1','mp'}, use_global_device_ids=true, to_apply=%region_26.27 | all-reduce | flops 1 | bytes 8 | tf_op jit(solution)/shard_map/psum | solution.py:248
  791.1 1.6 broadcast_in_dim_reshape.3
  (154 shorter events, 48.7 us)
Async XLA Ops:
  7.2 0.8 copy-start
  7.2 258.5 %all-gather.5.cloned.1.call-start = ((), (), s32[]{:S(2)}) async-start(), calls=%async_computation.15 | async-start | bytes 8650752 | tf_op jit(solution)/shard_map/all_gather | solution.py:152
  7.9 344.2 %all-gather.7.cloned.1.call-start = ((), (), s32[]{:S(2)}) async-start(), calls=%async_computation.16 | async-start | bytes 25952256 | tf_op jit(solution)/shard_map/all_gather | solution.py:166
  11.9 376.2 %all-gather.9.cloned.1.call-start = ((), (), s32[]{:S(2)}) async-start(), calls=%async_computation.17 | async-start | bytes 17301504 | tf_op jit(solution)/shard_map/all_gather | solution.py:169
  18.5 14.8 %copy-start.9 = (bf16[3,32,256]{2,1,0:T(8,128)(2,1)S(1)}, bf16[3,32,256]{2,1,0:T(8,128)(2,1)}, u32[]{:S(2)}) copy-start(bf16[3,32,256]{2,1,0:T(8,128)(2,1)} %param.29) | copy-start | bytes 147460
  18.5 14.8 %copy-start.10 = (bf16[256,32]{0,1:T(8,128)(2,1)S(1)}, bf16[256,32]{0,1:T(8,128)(2,1)}, u32[]{:S(2)}) copy-start(bf16[256,32]{0,1:T(8,128)(2,1)} %param.30) | copy-start | bytes 49156
  18.5 14.9 %copy-start.7 = (bf16[32,1024]{1,0:T(8,128)(2,1)S(1)}, bf16[32,1024]{1,0:T(8,128)(2,1)}, u32[]{:S(2)}) copy-start(bf16[32,1024]{1,0:T(8,128)(2,1)} %param.31) | copy-start | bytes 196612
  18.5 14.9 %copy-start.8 = (bf16[1024,32]{0,1:T(8,128)(2,1)S(1)}, bf16[1024,32]{0,1:T(8,128)(2,1)}, u32[]{:S(2)}) copy-start(bf16[1024,32]{0,1:T(8,128)(2,1)} %param.32) | copy-start | bytes 196612
  36.8 10.1 %copy-start.2 = (bf16[512,1024]{1,0:T(8,128)(2,1)S(1)}, bf16[512,1024]{1,0:T(8,128)(2,1)}, u32[]{:S(2)}) copy-start(bf16[512,1024]{1,0:T(8,128)(2,1)} %param.18) | copy-start | bytes 3145732
  36.8 97.3 %all-to-all-start = ((bf16[32,32,3072]{2,1,0:T(8,128)(2,1)}), bf16[32,32,3072]{2,1,0:T(8,128)(2,1)}, u32[]{:S(2)}, u32[]{:S(2)}) async-start(bf16[32,32,3072]{2,1,0:T(8,128)(2,1)} %stack.2), calls=%async_computation | async-start | bytes 12582912 | tf_op jit(solution)/shard_map/all_to_all | solution.py:150
  46.9 0.7 copy-start.12
  46.9 0.7 copy-start.13
  208.4 5.0 copy-start.3
  208.4 46.7 %all-to-all-start.2 = ((bf16[4,512,1024]{2,1,0:T(8,128)(2,1)}), bf16[4,512,1024]{2,1,0:T(8,128)(2,1)}, u32[]{:S(2)}, u32[]{:S(2)}) async-start(bf16[4,512,1024]{2,1,0:T(8,128)(2,1)} %broadcast_in_dim.45), calls=%async_computation.2 | async-start | bytes 8388608 | tf_op jit(solution)/shard_map/all_to_all | solution.py:46
  213.4 2.1 copy-start.14
  213.4 2.8 copy-start.15
  255.1 16.2 %all-to-all-start.4 = ((bf16[4,128,1024]{2,1,0:T(8,128)(2,1)}), bf16[4,128,1024]{2,1,0:T(8,128)(2,1)}, u32[]{:S(2)}, u32[]{:S(2)}) async-start(bf16[4,128,1024]{2,1,0:T(8,128)(2,1)} %bitcast.237), calls=%async_computation.4 | async-start | bytes 2097152 | tf_op jit(solution)/shard_map/all_to_all | solution.py:172
  271.3 24.3 %all-to-all-start.3 = ((bf16[4,64,1024]{2,1,0:T(8,128)(2,1)}), bf16[4,64,1024]{2,1,0:T(8,128)(2,1)S(1)}, u32[]{:S(2)}, u32[]{:S(2)}) async-start(bf16[4,64,1024]{2,1,0:T(8,128)(2,1)} %bitcast.21), calls=%async_computation.3 | async-start | bytes 1048576 | tf_op jit(solution)/shard_map/all_to_all | solution.py:205
  300.1 48.9 %all-to-all-start.5 = ((bf16[4,512,1024]{1,2,0:T(8,128)(2,1)}), bf16[4,512,1024]{1,2,0:T(8,128)(2,1)}, u32[]{:S(2)}, u32[]{:S(2)}) async-start(bf16[4,512,1024]{1,2,0:T(8,128)(2,1)} %broadcast_in_dim.46), calls=%async_computation.5 | async-start | bytes 8388608 | tf_op jit(solution)/shard_map/all_to_all | solution.py:46
  305.6 1.2 copy-start.11
  383.6 24.2 %all-to-all-start.6 = ((bf16[4,512,512]{1,2,0:T(8,128)(2,1)}), bf16[4,512,512]{1,2,0:T(8,128)(2,1)}, u32[]{:S(2)}, u32[]{:S(2)}) async-start(bf16[4,512,512]{1,2,0:T(8,128)(2,1)} %broadcast_in_dim.49), calls=%async_computation.6 | async-start | bytes 4194304 | tf_op jit(solution)/shard_map/all_to_all | solution.py:46
  415.5 46.2 %slice-start.4 = ((s8[6291456]{0:T(1024)(128)(4,1)}), s8[4194304]{0:T(1024)(128)(4,1)S(1)}, s32[]{:S(2)}) async-start(s8[6291456]{0:T(1024)(128)(4,1)} %bitcast.252), calls=%async_computation.22 | async-start | bytes 8388608
  415.9 45.9 %slice-start.5 = ((s8[6291456]{0:T(1024)(128)(4,1)}), s8[2097152]{0:T(1024)(128)(4,1)S(1)}, s32[]{:S(2)}) async-start(s8[6291456]{0:T(1024)(128)(4,1)} %bitcast.252), calls=%async_computation.23 | async-start | bytes 4194304
  475.6 22.5 %all-to-all-start.9 = ((bf16[4,512,512]{1,2,0:T(8,128)(2,1)}), bf16[4,512,512]{1,2,0:T(8,128)(2,1)}, u32[]{:S(2)}, u32[]{:S(2)}) async-start(bf16[4,512,512]{1,2,0:T(8,128)(2,1)} %broadcast_in_dim.53), calls=%async_computation.9 | async-start | bytes 4194304 | tf_op jit(solution)/shard_map/all_to_all | solution.py:46
  480.1 18.0 %copy-start.4 = (bf16[512,1024]{1,0:T(8,128)(2,1)S(1)}, bf16[512,1024]{1,0:T(8,128)(2,1)}, u32[]{:S(2)}) copy-start(bf16[512,1024]{1,0:T(8,128)(2,1)} %add_convert_fusion.3) | copy-start | bytes 3145732
  503.3 1.0 copy-start.5
  503.8 43.9 %slice-start.2 = ((s8[6291456]{0:T(1024)(128)(4,1)}), s8[4194304]{0:T(1024)(128)(4,1)S(1)}, s32[]{:S(2)}) async-start(s8[6291456]{0:T(1024)(128)(4,1)} %bitcast.249), calls=%async_computation.20 | async-start | bytes 8388608
  504.3 43.5 %slice-start.3 = ((s8[6291456]{0:T(1024)(128)(4,1)}), s8[2097152]{0:T(1024)(128)(4,1)S(1)}, s32[]{:S(2)}) async-start(s8[6291456]{0:T(1024)(128)(4,1)} %bitcast.249), calls=%async_computation.21 | async-start | bytes 4194304
  561.7 20.4 %all-to-all-start.11 = ((bf16[4,512,512]{1,2,0:T(8,128)(2,1)}), bf16[4,512,512]{1,2,0:T(8,128)(2,1)}, u32[]{:S(2)}, u32[]{:S(2)}) async-start(bf16[4,512,512]{1,2,0:T(8,128)(2,1)} %broadcast_in_dim.55), calls=%async_computation.11 | async-start | bytes 4194304 | tf_op jit(solution)/shard_map/all_to_all | solution.py:46
  566.1 15.9 %copy-start.6 = (bf16[512,1024]{1,0:T(8,128)(2,1)S(1)}, bf16[512,1024]{1,0:T(8,128)(2,1)}, u32[]{:S(2)}) copy-start(bf16[512,1024]{1,0:T(8,128)(2,1)} %copy-done.5) | copy-start | bytes 3145732
  587.8 41.7 %slice-start = ((s8[6291456]{0:T(1024)(128)(4,1)}), s8[4194304]{0:T(1024)(128)(4,1)S(1)}, s32[]{:S(2)}) async-start(s8[6291456]{0:T(1024)(128)(4,1)} %bitcast.246), calls=%async_computation.18 | async-start | bytes 8388608
  588.2 41.4 %slice-start.1 = ((s8[6291456]{0:T(1024)(128)(4,1)}), s8[2097152]{0:T(1024)(128)(4,1)S(1)}, s32[]{:S(2)}) async-start(s8[6291456]{0:T(1024)(128)(4,1)} %bitcast.246), calls=%async_computation.19 | async-start | bytes 4194304
  643.5 18.9 %all-to-all-start.13 = ((bf16[4,512,512]{1,2,0:T(8,128)(2,1)}), bf16[4,512,512]{1,2,0:T(8,128)(2,1)S(1)}, u32[]{:S(2)}, u32[]{:S(2)}) async-start(bf16[4,512,512]{1,2,0:T(8,128)(2,1)} %broadcast_in_dim.57), calls=%async_computation.13 | async-start | bytes 4194304 | tf_op jit(solution)/shard_map/all_to_all | solution.py:46
  668.0 3.7 copy-start.16
  668.0 122.4 %all-to-all-start.14 = ((bf16[4,128,1024]{2,1,0:T(8,128)(2,1)}), bf16[4,128,1024]{2,1,0:T(8,128)(2,1)S(1)}, u32[]{:S(2)}, u32[]{:S(2)}) async-start(bf16[4,128,1024]{2,1,0:T(8,128)(2,1)} %bitcast.274), calls=%async_computation.14 | async-start | bytes 2097152 | tf_op jit(solution)/shard_map/all_to_all | solution.py:240
  790.3 2.4 copy-start.1
Sparse Core Ops, SparseCore 0:
  10.2 116.0 all-gather.4
  128.6 98.6 all-gather.6
  229.6 77.5 all-gather.8
